TPU v7x, 256 devices: a whole 4x4x8 slice. The times are simulated.
256 devices in a mesh: expert: 16 (over x, y), dp: 16 (over z, core).
Axes of the slice: x: 4, y: 4, z: 8, core: 2. Of those that a mesh axis runs over, the one named last changes fastest.
Arguments:
- tokens: bfloat16 [2, 32768, 1280], P(None, ('expert', 'dp')), may hold values from -6 to 6
- modality: int32 [2, 32768], P(None, ('expert', 'dp')), may hold values from 0 to 1, as said below
- routes: int32 [2, 32768, 1], P(None, ('expert', 'dp')), may hold values from 0 to 15; in each aligned block of 128 rows (0 to 127, 128 to 255, ..., all dimensions but the last counted through in order) at most 16 rows name the same one
- router: bfloat16 [1280, 16], replicated, may hold values from -0.15625 to 0.15625
- w_in: bfloat16 [16, 1280, 5120], P('expert', 'dp'), may hold values from -0.15625 to 0.15625
- w_out: bfloat16 [16, 5120, 1280], P('expert', 'dp'), may hold values from -0.078125 to 0.078125
Outputs:
- mixed: bfloat16 [2, 32768, 1280], P(None, ('expert', 'dp'))
- load: float32 [2, 2, 16], replicated
Inputs may be any that keep to these rules, and one draw needn't show every extreme that they name: `routes`: among the 128 tokens of one micro-batch on one device (aligned blocks of 128 rows), at most 16 are routed to any one expert. `modality`: in every aligned block of 128 tokens of a micro-batch, the number of text tokens lies between 32 and 96.
All inputs are finite; a program needn't handle non-finite values.
Results may differ from a plain program's by a relative error of at most 0.0057.
Values may be sent and summed in bfloat16 or wider, within the bound.
No kernel may reach another device: no remote copies, remote signals or barrier semaphores. Data moves between devices by JAX's collectives and lax.ppermute only.
A program may use at most 192 MiB of HBM per device.

v0:
```python
import jax
import jax.numpy as jnp
from jax import lax
from jax.sharding import Mesh
from jax.sharding import PartitionSpec as P

EXPERT = ("expert_0", "expert_1")
DP = ("dp_0", "dp_1")
EXPERT_DP = ("expert_0", "expert_1", "dp_0", "dp_1")


def over_axes(shard, axes):
    for axis in axes:
        shard = lax.psum(shard, axis)
    return shard


def on_device(tokens, modality, routes, router, w_in, w_out):
    micro_count, tok_count, model_width = tokens.shape
    experts = router.shape[1]
    capacity = 2 * tok_count // experts
    logits = jnp.einsum("mtd,de->mte", tokens, router, preferred_element_type=jnp.float32)
    onehot = (routes == jnp.arange(experts, dtype=jnp.int32)[None, None, :]).astype(jnp.float32)
    gating = jax.nn.sigmoid(jnp.sum(logits * onehot, axis=-1))
    running = jnp.cumsum(onehot, axis=1)
    slot_pos = jnp.sum((running - 1.0) * onehot, axis=-1)
    slot_hot = (
        slot_pos[:, :, None] == jnp.arange(capacity, dtype=jnp.float32)[None, None, :]
    ).astype(jnp.float32)
    placer = (onehot[:, :, :, None] * slot_hot[:, :, None, :]).reshape(
        micro_count, tok_count, experts * capacity
    )
    placer = placer.astype(jnp.bfloat16)
    buffer = jnp.einsum("mtk,mtd->mkd", placer, tokens, preferred_element_type=jnp.float32)
    buffer = buffer.astype(jnp.bfloat16).reshape(micro_count, experts, capacity, model_width)
    arrived = lax.all_to_all(buffer, EXPERT, split_axis=1, concat_axis=1, tiled=True)
    token_rows = arrived.reshape(-1, model_width)
    columns = token_rows
    pre_act = jnp.dot(
        columns, lax.all_gather(w_in, DP, axis=1, tiled=True)[0], preferred_element_type=jnp.float32
    )
    hidden = jax.nn.gelu(pre_act, approximate=True).astype(jnp.bfloat16)
    columns = hidden
    served = jnp.dot(
        columns,
        lax.all_gather(w_out, DP, axis=1, tiled=True)[0],
        preferred_element_type=jnp.float32,
    )
    served = served.astype(jnp.bfloat16).reshape(arrived.shape)
    returned = lax.all_to_all(served, EXPERT, split_axis=1, concat_axis=1, tiled=True)
    returned = returned.reshape(micro_count, experts * capacity, model_width)
    combined = jnp.einsum("mtk,mkd->mtd", placer, returned, preferred_element_type=jnp.float32)
    mixed = (combined * gating[:, :, None]).astype(jnp.bfloat16)
    exps = jnp.exp(logits)
    router_probs = exps / jnp.sum(exps, axis=-1, keepdims=True)
    modal_hot = (modality[:, :, None] == jnp.arange(2, dtype=jnp.int32)[None, None, :]).astype(
        jnp.float32
    )
    counts = jnp.einsum("mtk,mte->ke", modal_hot, onehot, precision=lax.Precision.HIGHEST)
    prob_sums = jnp.einsum("mtk,mte->ke", modal_hot, router_probs, precision=lax.Precision.HIGHEST)
    modal_counts = jnp.sum(modal_hot, axis=(0, 1))
    counts, prob_sums, modal_counts = (
        over_axes(counts, EXPERT_DP),
        over_axes(prob_sums, EXPERT_DP),
        over_axes(modal_counts, EXPERT_DP),
    )
    load = jnp.stack(
        [experts * counts / modal_counts[:, None], experts * prob_sums / modal_counts[:, None]]
    )
    return (mixed, load)


def solution(mesh):
    torus = Mesh(mesh.devices.reshape(4, 4, 8, 2), ("expert_0", "expert_1", "dp_0", "dp_1"))
    in_specs = (
        P(None, EXPERT_DP, None),
        P(None, EXPERT_DP),
        P(None, EXPERT_DP, None),
        P(),
        P(EXPERT, DP, None),
        P(EXPERT, DP, None),
    )
    out_specs = (P(None, EXPERT_DP, None), P())
    return jax.shard_map(
        on_device, mesh=torus, in_specs=in_specs, out_specs=out_specs, check_vma=False
    )
```

profile of v0, /device:TPU:1, one launch (start us, length us, event | category | flops | bytes accessed | tf_op | source)
XLA Modules:
  0.0 258.7 jit_solution(4837752513307506845)
XLA Ops:
  7.2 0.0 copy-start
  7.2 0.0 all-gather.5.cloned.1.call-start
  7.2 0.7 all-gather.5.cloned.1.call-update
  7.9 0.0 all-gather.3.cloned.1.call-start
  8.0 0.7 all-gather.3.cloned.1.call-update
  8.7 0.7 fusion.30
  9.3 0.1 copy.21
  9.5 0.2 reduce_window_sum.11
  9.6 0.1 copy.22
  9.7 0.8 fusion.29
  10.5 0.0 copy-done
  10.5 0.5 convolution_convert_fusion
  11.0 0.1 copy.23
  11.1 26.3 %all_to_all.10 = bf16[2,16,16,1280]{3,2,0,1:T(8,128)(2,1)S(1)} all-to-all(bf16[2,16,16,1280]{3,2,0,1:T(8,128)(2,1)S(1)} %copy.23), channel_id=1, replica_groups=mesh['expert_0'=4,'expert_1'=4,'dp_0'=8,'dp_1'=2] {'expert_0','expert_1'}, dimensions={1} | all-to-all | bytes 2621440 | tf_op jit(solution)/shard_map/all_to_all | solution.py:36
  37.5 0.1 copy.24
  37.6 54.6 %all-gather.5.cloned.1.call-done = bf16[1,5120,1280]{2,1,0:T(8,128)(2,1)} async-done(((bf16[1,320,1280]{2,1,0:T(8,128)(2,1)}), bf16[1,5120,1280]{2,1,0:T(8,128)(2,1)}) %all-gather.5.cloned.1.call-update) | async-done | bytes 13107216 | tf_op jit(solution)/shard_map/all_gather | solution.py:46
  92.1 78.5 %all-gather.3.cloned.1.call-done = bf16[1,1280,5120]{2,1,0:T(8,128)(2,1)} async-done(((bf16[1,80,5120]{2,1,0:T(8,128)(2,1)}), bf16[1,1280,5120]{2,1,0:T(8,128)(2,1)}) %all-gather.3.cloned.1.call-update) | async-done | bytes 13107216 | tf_op jit(solution)/shard_map/all_gather | solution.py:40
  170.6 22.4 %fusion.20 = bf16[512,1280]{1,0:T(8,128)(2,1)S(1)} fusion(bf16[1,5120,1280]{2,1,0:T(8,128)(2,1)} %all-gather.5.cloned.1.call-done, bf16[512,1280]{1,0:T(8,128)(2,1)S(1)} %bitcast.41, bf16[1,1280,5120]{2,1,0:T(8,128)(2,1)} %all-gather.3.cloned.1.call-done), kind=kOutput, calls=%fused_computation.17 | convolution fusion | flops 13446021120 | bytes 28835840 | tf_op jit(solution)/shard_map/dot_general | solution.py:44
  193.0 0.0 copy-start.3
  193.0 0.0 copy-start.2
  193.0 0.0 copy-start.1
  193.0 1.2 copy.25
  194.2 6.5 %all-to-all-start.1 = ((bf16[2,16,16,1280]{3,2,0,1:T(8,128)(2,1)}), bf16[2,16,16,1280]{3,2,0,1:T(8,128)(2,1)S(1)}, u32[]{:S(2)}, u32[]{:S(2)}) async-start(bf16[2,16,16,1280]{3,2,0,1:T(8,128)(2,1)} %copy.25), calls=%async_computation.1 | async-start | bytes 2621440 | tf_op jit(solution)/shard_map/all_to_all | solution.py:50
  200.8 0.0 copy-done.3
  200.8 0.1 convert_reduce_fusion
  200.9 0.0 copy-done.2
  200.9 0.1 convolution_bitcast_fusion.1
  201.0 0.0 copy-done.1
  201.0 0.3 exponential_reduce_fusion
  201.4 0.1 convolution_bitcast_fusion
  201.5 18.4 %all-reduce.2 = (f32[2,16]{1,0:T(2,128)S(1)}, f32[2]{0:T(128)S(1)}, f32[2,16]{1,0:T(2,128)S(1)}) all-reduce(f32[2,16]{1,0:T(2,128)S(1)} %convolution_bitcast_fusion, f32[2]{0:T(128)S(1)} %convert_reduce_fusion, f32[2,16]{1,0:T(2,128)S(1)} %convolution_bitcast_fusion.1), channel_id=1, replica_groups=mesh['expert_0'=4,'expert_1'=4,'dp_0'=8,'dp_1'=2] {'expert_0'}, use_global_device_ids=true, to_apply=%region_13.14 | all-reduce | flops 66 | bytes 528 | tf_op jit(solution)/shard_map/psum | solution.py:14
  219.9 8.1 %all-reduce.1 = (f32[2,16]{1,0:T(2,128)S(1)}, f32[2]{0:T(128)S(1)}, f32[2,16]{1,0:T(2,128)S(1)}) all-reduce(f32[2,16]{1,0:T(2,128)S(1)} %get-tuple-element.10, f32[2]{0:T(128)S(1)} %get-tuple-element.11, f32[2,16]{1,0:T(2,128)S(1)} %get-tuple-element.12), channel_id=1, replica_groups=mesh['expert_0'=4,'expert_1'=4,'dp_0'=8,'dp_1'=2] {'expert_1'}, use_global_device_ids=true, to_apply=%region_14.15 | all-reduce | flops 66 | bytes 528 | tf_op jit(solution)/shard_map/psum | solution.py:14
  227.9 11.8 %all-reduce = (f32[2,16]{1,0:T(2,128)S(1)}, f32[2]{0:T(128)S(1)}, f32[2,16]{1,0:T(2,128)S(1)}) all-reduce(f32[2,16]{1,0:T(2,128)S(1)} %get-tuple-element.7, f32[2]{0:T(128)S(1)} %get-tuple-element.8, f32[2,16]{1,0:T(2,128)S(1)} %get-tuple-element.9), channel_id=1, replica_groups=mesh['expert_0'=4,'expert_1'=4,'dp_0'=8,'dp_1'=2] {'dp_0'}, use_global_device_ids=true, to_apply=%region_15.16 | all-reduce | flops 66 | bytes 528 | tf_op jit(solution)/shard_map/psum | solution.py:14
  239.7 10.2 %all-reduce.3 = (f32[2,16]{1,0:T(2,128)S(1)}, f32[2]{0:T(128)S(1)}, f32[2,16]{1,0:T(2,128)S(1)}) all-reduce(f32[2,16]{1,0:T(2,128)S(1)} %get-tuple-element.4, f32[2]{0:T(128)S(1)} %get-tuple-element.5, f32[2,16]{1,0:T(2,128)S(1)} %get-tuple-element.6), channel_id=1, replica_groups=mesh['expert_0'=4,'expert_1'=4,'dp_0'=8,'dp_1'=2] {'dp_1'}, use_global_device_ids=true, to_apply=%region_16.17 | all-reduce | flops 66 | bytes 528 | tf_op jit(solution)/shard_map/psum | solution.py:14
  249.9 0.1 divide_bitcast_fusion.1
  249.9 0.6 pad_maximum_fusion
  250.5 0.0 all-to-all-done.1
  250.5 0.1 copy.26
  250.6 1.2 fusion.25
  (2 shorter events, 0.0 us)
Async XLA Ops:
  7.2 3.3 %copy-start = (bf16[2,128,1280]{2,1,0:T(8,128)(2,1)S(1)}, bf16[2,128,1280]{2,1,0:T(8,128)(2,1)}, u32[]{:S(2)}) copy-start(bf16[2,128,1280]{2,1,0:T(8,128)(2,1)} %param.6) | copy-start | bytes 1966084
  7.2 84.9 %all-gather.5.cloned.1.call-start = ((), (), s32[]{:S(2)}) async-start(), calls=%async_computation.3 | async-start | bytes 13926400 | tf_op jit(solution)/shard_map/all_gather | solution.py:46
  7.9 162.7 %all-gather.3.cloned.1.call-start = ((), (), s32[]{:S(2)}) async-start(), calls=%async_computation.2 | async-start | bytes 13926400 | tf_op jit(solution)/shard_map/all_gather | solution.py:40
  193.0 7.8 %copy-start.3 = (s32[2,128]{1,0:T(2,128)S(1)}, s32[2,128]{1,0:T(2,128)}, u32[]{:S(2)}) copy-start(s32[2,128]{1,0:T(2,128)} %param.7) | copy-start | bytes 3076
  193.0 7.9 %copy-start.2 = (s32[2,128,1]{1,2,0:T(1,128)S(1)}, s32[2,128,1]{1,2,0:T(1,128)}, u32[]{:S(2)}) copy-start(s32[2,128,1]{1,2,0:T(1,128)} %param.8) | copy-start | bytes 3076
  193.0 8.0 %copy-start.1 = (bf16[1280,16]{0,1:T(8,128)(2,1)S(1)}, bf16[1280,16]{0,1:T(8,128)(2,1)}, u32[]{:S(2)}) copy-start(bf16[1280,16]{0,1:T(8,128)(2,1)} %param.9) | copy-start | bytes 122884
  194.2 56.3 %all-to-all-start.1 = ((bf16[2,16,16,1280]{3,2,0,1:T(8,128)(2,1)}), bf16[2,16,16,1280]{3,2,0,1:T(8,128)(2,1)S(1)}, u32[]{:S(2)}, u32[]{:S(2)}) async-start(bf16[2,16,16,1280]{3,2,0,1:T(8,128)(2,1)} %copy.25), calls=%async_computation.1 | async-start | bytes 2621440 | tf_op jit(solution)/shard_map/all_to_all | solution.py:50
Sparse Core Ops, SparseCore 0:
  9.8 82.2 all-gather.4
  93.9 76.5 all-gather.2
where the time goes:
time: 259 us
  waiting for transfers between devices  134 us (52%)
  blocking collectives  74.7 us (29%)
  matrix products  24.7 us (10%)
  between operations  14.2 us (5%)
  starting transfers between devices  6.6 us (3%)
    all_gather x1, waiting for transfers between devices, on_device(): lax.all_gather(w_in, DP, axis=1, tiled=True)[0]  78.5 us
    all_gather x1, waiting for transfers between devices, on_device(): lax.all_gather(w_out, DP, axis=1, tiled=True)[0]  54.6 us
    psum x4, blocking collectives, over_axes(): shard = lax.psum(shard, axis)  48.4 us
    all_to_all x1, blocking collectives, on_device(): lax.all_to_all(buffer, EXPERT, split_axis=1, concat_axis=1, tiled=True)  26.3 us
    dot_general x1, matrix products, on_device(): jnp.dot(columns, lax.all_gather(w_out, DP, axis=1, tiled=True)[0], prefer...  22.4 us
    all_to_all x1, starting transfers between devices, on_device(): lax.all_to_all(served, EXPERT, split_axis=1, concat_axis=1, tiled=True)  6.52 us
  transfers between devices with their start and end apart: 3, of which 2 were waited for; matrix products, arithmetic and copies ran while one was open for 2% of the time, Pallas kernels for 0%

commit v1 on v0

--- a/solution.py
+++ b/solution.py
@@ -37,7 +37,9 @@
     token_rows = arrived.reshape(-1, model_width)
     columns = token_rows
     pre_act = jnp.dot(
-        columns, lax.all_gather(w_in, DP, axis=1, tiled=True)[0], preferred_element_type=jnp.float32
+        columns,
+        jnp.concatenate(lax.all_to_all(jnp.stack([w_in] * lax.axis_size(DP)), DP, 0, 0), axis=1)[0],
+        preferred_element_type=jnp.float32,
     )
     hidden = jax.nn.gelu(pre_act, approximate=True).astype(jnp.bfloat16)
     columns = hidden

time: 259 us -> 486 us (1.88)
  waiting for transfers between devices: 134 us -> 346 us
  local copies, waits for them, and re-layouts: 1.69 us -> 9.21 us
  starting transfers between devices: 6.6 us -> 14.1 us
    all_to_all x0 -> x1, waiting for transfers between devices: none -> 345 us  [on_device(): lax.all_to_all(jnp.stack([w_in] * lax.axis_size(DP)), DP, 0, 0)]
    all_gather x1 -> x0, waiting for transfers between devices: 78.5 us -> none  [on_device(): lax.all_gather(w_in, DP, axis=1, tiled=True)[0]]
    all_gather x1, waiting for transfers between devices: 54.6 us -> 0.01 us  [on_device(): lax.all_gather(w_out, DP, axis=1, tiled=True)[0]]
    all_to_all x0 -> x1, starting transfers between devices: none -> 10.2 us  [on_device(): lax.all_to_all(jnp.stack([w_in] * lax.axis_size(DP)), DP, 0, 0)]
    another operation x0 -> x1, local copies, waits for them, and re-layouts: none -> 7.51 us  [on_device(): jnp.stack([w_in] * lax.axis_size(DP))]
  transfers between devices with their start and end apart: 3 -> 3, of which waited for: 2 -> 1; matrix products, arithmetic and copies ran while one was open for 2% -> 0% of each run, Pallas kernels for 0% -> 0%
where the time goes in v1:
time: 486 us; the launch traced here: 485 us
  waiting for transfers between devices  346 us (71%)
  blocking collectives  74.9 us (15%)
  matrix products  24.8 us (5%)
  starting transfers between devices  14.1 us (3%)
  between operations  14.1 us (3%)
  local copies, waits for them, and re-layouts  9.21 us (2%)
    all_to_all x1, waiting for transfers between devices, on_device(): lax.all_to_all(jnp.stack([w_in] * lax.axis_size(DP)), DP, 0, 0)  345 us
    psum x4, blocking collectives, over_axes(): shard = lax.psum(shard, axis)  48.5 us
    all_to_all x1, blocking collectives, on_device(): lax.all_to_all(buffer, EXPERT, split_axis=1, concat_axis=1, tiled=True)  26.3 us
    dot_general x1, matrix products, on_device(): jnp.dot(columns, lax.all_gather(w_out, DP, axis=1, tiled=True)[0], prefer...  22.5 us
    all_to_all x1, starting transfers between devices, on_device(): lax.all_to_all(jnp.stack([w_in] * lax.axis_size(DP)), DP, 0, 0)  10.2 us
  transfers between devices with their start and end apart: 3, of which 1 were waited for; matrix products, arithmetic and copies ran while one was open for 0% of the time, Pallas kernels for 0%

profile of v1, /device:TPU:1, one launch (start us, length us, event | category | flops | bytes accessed | tf_op | source)
XLA Modules:
  0.0 485.2 jit_solution(8394417171505198803)
XLA Ops:
  7.2 0.0 copy-start
  7.2 0.8 fusion.25
  7.9 0.1 copy.21
  8.0 0.2 reduce_window_sum.11
  8.2 0.1 copy.22
  8.3 0.8 fusion.24
  9.1 0.0 copy-done
  9.1 0.5 convolution_convert_fusion
  9.6 0.1 copy.23
  9.7 26.3 %all_to_all.15 = bf16[2,16,16,1280]{3,2,0,1:T(8,128)(2,1)S(1)} all-to-all(bf16[2,16,16,1280]{3,2,0,1:T(8,128)(2,1)S(1)} %copy.23), channel_id=1, replica_groups=mesh['expert_0'=4,'expert_1'=4,'dp_0'=8,'dp_1'=2] {'expert_0','expert_1'}, dimensions={1} | all-to-all | bytes 2621440 | tf_op jit(solution)/shard_map/all_to_all | solution.py:36
  36.1 7.5 %stack.8 = bf16[16,1,80,5120]{3,2,1,0:T(8,128)(2,1)} broadcast(bf16[80,5120]{1,0:T(8,128)(2,1)} %bitcast.39), dimensions={2,3} | broadcast | bytes 13926400 | tf_op jit(solution)/shard_map/stack | solution.py:41
  43.6 10.2 %all-to-all-start.1 = ((bf16[16,1,80,5120]{3,2,1,0:T(8,128)(2,1)}), bf16[16,1,80,5120]{3,2,1,0:T(8,128)(2,1)}, u32[]{:S(2)}, u32[]{:S(2)}) async-start(bf16[16,1,80,5120]{3,2,1,0:T(8,128)(2,1)} %stack.8), calls=%async_computation.1 | async-start | bytes 26214400 | tf_op jit(solution)/shard_map/all_to_all | solution.py:41
  53.8 0.2 all-gather.2.cloned.1.call-start
  54.0 0.5 all-gather.2.cloned.1.call-update
  54.5 0.1 copy.24
  54.6 345.0 %all-to-all-done.1 = bf16[16,1,80,5120]{3,2,1,0:T(8,128)(2,1)} async-done(((bf16[16,1,80,5120]{3,2,1,0:T(8,128)(2,1)}), bf16[16,1,80,5120]{3,2,1,0:T(8,128)(2,1)}, u32[]{:S(2)}, u32[]{:S(2)}) %all-to-all-start.1) | async-done | bytes 13107232 | tf_op jit(solution)/shard_map/all_to_all | solution.py:41
  399.7 0.0 all-gather.2.cloned.1.call-done
  399.7 0.0 copy-start.3
  399.7 0.0 copy-start.2
  399.7 0.0 copy-start.1
  399.7 22.5 %fusion.15 = bf16[512,1280]{1,0:T(8,128)(2,1)S(1)} fusion(bf16[1,5120,1280]{2,1,0:T(8,128)(2,1)} %all-gather.2.cloned.1.call-done, bf16[512,1280]{1,0:T(8,128)(2,1)S(1)} %bitcast.35, bf16[1280,5120]{1,0:T(8,128)(2,1)} %bitcast.5), kind=kOutput, calls=%fused_computation.15 | convolution fusion | flops 13446021120 | bytes 28835840 | tf_op jit(solution)/shard_map/dot_general | solution.py:46
  422.1 1.2 copy.25
  423.3 3.7 all-to-all-start.2
  427.0 0.0 copy-done.3
  427.1 0.1 convert_reduce_fusion
  427.2 0.0 copy-done.2
  427.2 0.1 convolution_bitcast_fusion.1
  427.3 0.0 copy-done.1
  427.3 0.3 exponential_reduce_fusion
  427.6 0.1 convolution_bitcast_fusion
  427.8 17.7 %all-reduce.2 = (f32[2,16]{1,0:T(2,128)S(1)}, f32[2]{0:T(128)S(1)}, f32[2,16]{1,0:T(2,128)S(1)}) all-reduce(f32[2,16]{1,0:T(2,128)S(1)} %convolution_bitcast_fusion, f32[2]{0:T(128)S(1)} %convert_reduce_fusion, f32[2,16]{1,0:T(2,128)S(1)} %convolution_bitcast_fusion.1), channel_id=1, replica_groups=mesh['expert_0'=4,'expert_1'=4,'dp_0'=8,'dp_1'=2] {'expert_0'}, use_global_device_ids=true, to_apply=%region_13.14 | all-reduce | flops 66 | bytes 528 | tf_op jit(solution)/shard_map/psum | solution.py:14
  445.4 8.6 %all-reduce.1 = (f32[2,16]{1,0:T(2,128)S(1)}, f32[2]{0:T(128)S(1)}, f32[2,16]{1,0:T(2,128)S(1)}) all-reduce(f32[2,16]{1,0:T(2,128)S(1)} %get-tuple-element.10, f32[2]{0:T(128)S(1)} %get-tuple-element.11, f32[2,16]{1,0:T(2,128)S(1)} %get-tuple-element.12), channel_id=1, replica_groups=mesh['expert_0'=4,'expert_1'=4,'dp_0'=8,'dp_1'=2] {'expert_1'}, use_global_device_ids=true, to_apply=%region_14.15 | all-reduce | flops 66 | bytes 528 | tf_op jit(solution)/shard_map/psum | solution.py:14
  454.0 12.3 %all-reduce = (f32[2,16]{1,0:T(2,128)S(1)}, f32[2]{0:T(128)S(1)}, f32[2,16]{1,0:T(2,128)S(1)}) all-reduce(f32[2,16]{1,0:T(2,128)S(1)} %get-tuple-element.7, f32[2]{0:T(128)S(1)} %get-tuple-element.8, f32[2,16]{1,0:T(2,128)S(1)} %get-tuple-element.9), channel_id=1, replica_groups=mesh['expert_0'=4,'expert_1'=4,'dp_0'=8,'dp_1'=2] {'dp_0'}, use_global_device_ids=true, to_apply=%region_15.16 | all-reduce | flops 66 | bytes 528 | tf_op jit(solution)/shard_map/psum | solution.py:14
  466.4 9.9 %all-reduce.3 = (f32[2,16]{1,0:T(2,128)S(1)}, f32[2]{0:T(128)S(1)}, f32[2,16]{1,0:T(2,128)S(1)}) all-reduce(f32[2,16]{1,0:T(2,128)S(1)} %get-tuple-element.4, f32[2]{0:T(128)S(1)} %get-tuple-element.5, f32[2,16]{1,0:T(2,128)S(1)} %get-tuple-element.6), channel_id=1, replica_groups=mesh['expert_0'=4,'expert_1'=4,'dp_0'=8,'dp_1'=2] {'dp_1'}, use_global_device_ids=true, to_apply=%region_16.17 | all-reduce | flops 66 | bytes 528 | tf_op jit(solution)/shard_map/psum | solution.py:14
  476.3 0.1 divide_bitcast_fusion.1
  476.4 0.6 pad_maximum_fusion
  477.0 0.0 all-to-all-done.2
  477.0 0.1 copy.26
  477.1 1.2 fusion.20
  (2 shorter events, 0.0 us)
Async XLA Ops:
  7.2 1.9 copy-start
  43.6 356.1 %all-to-all-start.1 = ((bf16[16,1,80,5120]{3,2,1,0:T(8,128)(2,1)}), bf16[16,1,80,5120]{3,2,1,0:T(8,128)(2,1)}, u32[]{:S(2)}, u32[]{:S(2)}) async-start(bf16[16,1,80,5120]{3,2,1,0:T(8,128)(2,1)} %stack.8), calls=%async_computation.1 | async-start | bytes 26214400 | tf_op jit(solution)/shard_map/all_to_all | solution.py:41
  53.8 345.9 %all-gather.2.cloned.1.call-start = ((), (), s32[]{:S(2)}) async-start(), calls=%async_computation.3 | async-start | bytes 13926400 | tf_op jit(solution)/shard_map/all_gather | solution.py:48
  399.7 27.4 %copy-start.3 = (s32[2,128]{1,0:T(2,128)S(1)}, s32[2,128]{1,0:T(2,128)}, u32[]{:S(2)}) copy-start(s32[2,128]{1,0:T(2,128)} %param.7) | copy-start | bytes 3076
  399.7 27.5 %copy-start.2 = (s32[2,128,1]{1,2,0:T(1,128)S(1)}, s32[2,128,1]{1,2,0:T(1,128)}, u32[]{:S(2)}) copy-start(s32[2,128,1]{1,2,0:T(1,128)} %param.8) | copy-start | bytes 3076
  399.7 27.6 %copy-start.1 = (bf16[1280,16]{0,1:T(8,128)(2,1)S(1)}, bf16[1280,16]{0,1:T(8,128)(2,1)}, u32[]{:S(2)}) copy-start(bf16[1280,16]{0,1:T(8,128)(2,1)} %param.9) | copy-start | bytes 122884
  423.3 53.7 %all-to-all-start.2 = ((bf16[2,16,16,1280]{3,2,0,1:T(8,128)(2,1)}), bf16[2,16,16,1280]{3,2,0,1:T(8,128)(2,1)S(1)}, u32[]{:S(2)}, u32[]{:S(2)}) async-start(bf16[2,16,16,1280]{3,2,0,1:T(8,128)(2,1)} %copy.25), calls=%async_computation.2 | async-start | bytes 2621440 | tf_op jit(solution)/shard_map/all_to_all | solution.py:52
Sparse Core Ops, SparseCore 0:
  56.4 261.9 all-gather.1
